TPU v7x, 32 devices: a whole 2x2x4 slice. The times are simulated.
32 devices in a mesh: group: 8 (over y, x, core), pos: 4 (over z).
Axes of the slice: x: 2, y: 2, z: 4, core: 2. Of those that a mesh axis runs over, the one named last changes fastest.
Arguments:
- features: bfloat16 [384, 256, 256], P(('group', 'pos')), may hold values from -6 to 6
- gain_attn: float32 [256], replicated, may hold values from 0.1 to 1.9
- w_query: bfloat16 [256, 256], replicated, as said below
- w_key: bfloat16 [256, 256], replicated, as said below
- w_value: bfloat16 [256, 256], replicated, may hold values from -0.375 to 0.375
- w_out: bfloat16 [256, 256], replicated, may hold values from -0.375 to 0.375
- gain_ffn: float32 [256], replicated, may hold values from 0.1 to 1.9
- w_up: bfloat16 [256, 1024], replicated, may hold values from -0.375 to 0.375
- w_down: bfloat16 [1024, 256], replicated, may hold values from -0.1875 to 0.1875
- counts: int32 [6], replicated, may hold values from 4 to 64, as said below
- offsets: int32 [6], replicated, may hold values from 0 to 380, as said below
Outputs:
- result: bfloat16 [384, 256, 256], P(('group', 'pos'))
Inputs may be any that keep to these rules, and one draw needn't show every extreme that they name: `counts`: each mixture has 4 to 64 groups, and one mixture has exactly 64. Mixture m occupies slots offsets[m] to offsets[m] + counts[m] - 1; the mixtures follow one another in order without intersection. `w_query`: a dense matrix of independent entries. `w_key`: a dense matrix of independent entries.
All inputs are finite; a program needn't handle non-finite values.
Results may differ from a plain program's by a relative error of at most 0.0065.
Values may be sent and summed in bfloat16 or wider, within the bound.
No kernel may reach another device: no remote copies, remote signals or barrier semaphores. Data moves between devices by JAX's collectives and lax.ppermute only.
A program may use at most 192 MiB of HBM per device.

v0:
```python
import math
import jax
import jax.numpy as jnp
from jax import lax
from jax.sharding import PartitionSpec as P

HEADS = 8
epsilon = 1e-05
masked_value = -1e30


def segment_ids(counts, offsets, slots_total):
    slots = jnp.arange(slots_total, dtype=jnp.int32)[:, None]
    inside = (slots >= offsets[None, :]) & (slots < offsets[None, :] + counts[None, :])
    labels = jnp.arange(counts.shape[0], dtype=jnp.int32)[None, :] + 1
    return jnp.sum(jnp.where(inside, labels, 0), axis=1) - 1


def layer_norm(values, gain):
    floats = values.astype(jnp.float32)
    average = jnp.mean(floats, axis=-1, keepdims=True)
    centred = floats - average
    spread = jnp.mean(centred * centred, axis=-1, keepdims=True)
    return (centred * lax.rsqrt(spread + epsilon) * gain).astype(jnp.bfloat16)


def feed_forward(middle, gain_ffn, w_up, w_down):
    second = layer_norm(middle, gain_ffn)
    hidden = jnp.maximum(jnp.dot(second, w_up, preferred_element_type=jnp.float32), 0.0).astype(
        jnp.bfloat16
    )
    return (
        middle.astype(jnp.float32) + jnp.dot(hidden, w_down, preferred_element_type=jnp.float32)
    ).astype(jnp.bfloat16)


def local(
    features, gain_attn, w_query, w_key, w_value, w_out, gain_ffn, w_up, w_down, counts, offsets
):
    group_devices = lax.axis_size("group")
    pos_devices = lax.axis_size("pos")
    local_groups = features.shape[0]
    width = features.shape[2]
    slots_total = local_groups * group_devices * pos_devices
    head_dim = width // HEADS
    scale = 1.0 / math.sqrt(head_dim)
    gathered = lax.all_to_all(features, ("group", "pos"), split_axis=1, concat_axis=0, tiled=True)
    owned = gathered.shape[1]
    labels = segment_ids(counts, offsets, slots_total)
    flat = gathered.reshape(slots_total * owned, width)
    normed = layer_norm(flat, gain_attn)

    def project(weight):
        product = jnp.dot(normed, weight, preferred_element_type=jnp.float32).astype(jnp.bfloat16)
        return product.reshape(slots_total, owned, HEADS, head_dim)

    query = project(w_query)
    keys = project(w_key)
    values = project(w_value)
    block = min(512, slots_total)

    def attend(start):
        block_query = lax.dynamic_slice_in_dim(query, start, block, 0)
        block_labels = lax.dynamic_slice_in_dim(labels, start, block, 0)
        scores = (
            jnp.einsum("qphe,kphe->phqk", block_query, keys, preferred_element_type=jnp.float32)
            * scale
        )
        allowed = (block_labels[:, None] == labels[None, :]) & (block_labels[:, None] >= 0)
        scores = jnp.where(allowed[None, None], scores, masked_value)
        highest = jnp.max(scores, axis=-1, keepdims=True)
        exponent = jnp.exp(scores - highest)
        total = jnp.sum(exponent, axis=-1, keepdims=True)
        weights = (exponent / total).astype(jnp.bfloat16)
        context = jnp.einsum(
            "phqk,kphe->qphe", weights, values, preferred_element_type=jnp.float32
        ).astype(jnp.bfloat16)
        return jnp.where((block_labels >= 0)[:, None, None, None], context, jnp.zeros_like(context))

    starts = jnp.arange(slots_total // block, dtype=jnp.int32) * block
    context = lax.map(attend, starts).reshape(slots_total * owned, width)
    middle = (
        flat.astype(jnp.float32) + jnp.dot(context, w_out, preferred_element_type=jnp.float32)
    ).astype(jnp.bfloat16)
    middle = middle.reshape(slots_total, owned, width)
    returned = lax.all_to_all(middle, ("group", "pos"), split_axis=0, concat_axis=1, tiled=True)
    finished = feed_forward(returned.reshape(-1, width), gain_ffn, w_up, w_down)
    return finished.reshape(returned.shape)


def solution(mesh):
    return jax.shard_map(
        local,
        mesh=mesh,
        in_specs=(
            P(("group", "pos"), None, None),
            P(),
            P(),
            P(),
            P(),
            P(),
            P(),
            P(),
            P(),
            P(),
            P(),
        ),
        out_specs=P(("group", "pos"), None, None),
        check_vma=False,
    )
```

profile of v0, /device:TPU:1, one launch (start us, length us, event | category | flops | bytes accessed | tf_op | source)
XLA Modules:
  0.0 253.2 jit_solution(11873321647180178728)
XLA Ops:
  0.0 0.0 copy-start
  0.0 0.0 copy-start.9
  0.0 0.0 copy-start.7
  0.0 3.7 %copy.33 = bf16[12,256,256]{2,0,1:T(8,128)(2,1)} copy(bf16[12,256,256]{2,1,0:T(8,128)(2,1)} %param.11) | data formatting | bytes 3145728 | tf_op args[0]
  3.8 7.1 %all-to-all-start = ((bf16[12,256,256]{2,0,1:T(8,128)(2,1)}), bf16[12,256,256]{2,0,1:T(8,128)(2,1)S(1)}, u32[]{:S(2)}, u32[]{:S(2)}) async-start(bf16[12,256,256]{2,0,1:T(8,128)(2,1)} %copy.33), calls=%async_computation | async-start | bytes 4194304 | tf_op jit(solution)/shard_map/all_to_all | solution.py:47
  10.8 0.0 copy-done.9
  10.9 0.0 copy-done.7
  10.9 0.1 select_reduce_fusion
  11.0 0.2 compare_and_fusion
  11.2 48.0 %all-to-all-done = bf16[12,256,256]{2,0,1:T(8,128)(2,1)S(1)} async-done(((bf16[12,256,256]{2,0,1:T(8,128)(2,1)}), bf16[12,256,256]{2,0,1:T(8,128)(2,1)S(1)}, u32[]{:S(2)}, u32[]{:S(2)}) %all-to-all-start) | async-done | bytes 1572896 | tf_op jit(solution)/shard_map/all_to_all | solution.py:47
  59.2 2.2 bitcast_reduce_fusion.1
  61.4 0.0 copy-start.5
  61.4 0.1 div.29
  61.5 2.8 %fusion.21 = f32[32,12,8]{2,1,0:T(8,128)S(1)} fusion(f32[12,32,8,256]{3,2,0,1:T(8,128)} %get-tuple-element.16, f32[32,12,8]{2,1,0:T(8,128)S(1)} %broadcast_multiply_fusion), kind=kLoop, calls=%fused_computation.36 | loop fusion | flops 2356224 | bytes 3170304 | tf_op jit(solution)/shard_map/reduce_sum | solution.py:23
  64.3 0.0 copy-start.1
  64.4 0.1 rsqrt.23
  64.5 0.0 copy-done.5
  64.5 3.1 %fusion.19 = bf16[3072,256]{1,0:T(8,128)(2,1)S(1)} fusion(f32[12,32,8,256]{3,2,0,1:T(8,128)} %get-tuple-element.16, f32[256]{0:T(256)S(1)} %copy-done.5, f32[3072]{0:T(1024)S(1)} %rsqrt.23, f32[3072]{0:T(1024)S(1)} %div.29), kind=kLoop, calls=%fused_computation.32 | loop fusion | flops 3145728 | bytes 4744192 | tf_op jit(solution)/shard_map/convert_element_type | solution.py:24
  67.6 0.0 copy-done.1
  67.6 1.7 convolution_convert_fusion.1
  69.4 0.0 copy-start.2
  69.4 7.9 %reshape.166 = bf16[384,8,8,32]{3,2,1,0:T(8,128)(2,1)} reshape(bf16[3072,256]{1,0:T(8,128)(2,1)} %convolution_convert_fusion.1) | data formatting | bytes 3145728 | tf_op jit(solution)/shard_map/reshape | solution.py:55
  77.2 0.0 copy-done.2
  77.2 1.7 convolution_convert_fusion
  78.9 0.0 copy-start.3
  78.9 7.9 %reshape.167 = bf16[384,8,8,32]{3,2,1,0:T(8,128)(2,1)} reshape(bf16[3072,256]{1,0:T(8,128)(2,1)} %convolution_convert_fusion) | data formatting | bytes 3145728 | tf_op jit(solution)/shard_map/reshape | solution.py:55
  86.8 0.0 copy-done.3
  86.8 1.7 convolution_convert_fusion.2
  88.5 7.9 %reshape.165 = bf16[384,8,8,32]{3,2,1,0:T(8,128)(2,1)} reshape(bf16[3072,256]{1,0:T(8,128)(2,1)} %convolution_convert_fusion.2) | data formatting | bytes 3145728 | tf_op jit(solution)/shard_map/reshape | solution.py:55
  96.4 22.9 %fusion.7 = f32[8,8,384,384]{2,3,1,0:T(8,128)} fusion(bf16[384,8,8,32]{3,2,1,0:T(8,128)(2,1)} %reshape.167, bf16[384,8,8,32]{3,2,1,0:T(8,128)(2,1)} %reshape.166), kind=kOutput, calls=%fused_computation.11 | convolution fusion | flops 603979776 | bytes 40894464 | tf_op jit(solution)/shard_map/while/body/eval_jaxpr/qphe,kphe->phqk/dot_general | solution.py:66
  119.3 42.9 %fusion.32 = (f32[8,8,384]{2,1,0:T(8,128)S(1)}, f32[8,8,384,384]{2,3,1,0:T(8,128)}) fusion(f32[8,8,384,384]{2,3,1,0:T(8,128)} %fusion.7, pred[384,384]{0,1:T(8,128)(4,1)S(1)} %compare_and_fusion), kind=kOutput, calls=%fused_computation.55 | output fusion | flops 56623488 | bytes 75743232 | tf_op jit(solution)/shard_map/while/body/eval_jaxpr/sub | solution.py:72
  162.3 17.4 %select_bitcast_fusion = bf16[384,8,8,32]{0,3,2,1:T(8,128)(2,1)S(1)} fusion(pred[384]{0:T(512)(128)(4,1)S(1)} %broadcast_compare_fusion, f32[8,8,384,384]{2,3,1,0:T(8,128)} %get-tuple-element.24, f32[8,8,384]{2,1,0:T(8,128)S(1)} %get-tuple-element.17, bf16[384,8,8,32]{3,2,1,0:T(8,128)(2,1)} %reshape.165), kind=kOutput, calls=%fused_computation.38 | convolution fusion | flops 624427008 | bytes 40993152 | tf_op jit(solution)/shard_map/while/body/eval_jaxpr/phqk,kphe->qphe/dot_general | solution.py:75
  179.7 9.3 %copy.39 = bf16[384,8,8,32]{3,2,1,0:T(8,128)(2,1)} copy(bf16[384,8,8,32]{0,3,2,1:T(8,128)(2,1)S(1)} %select_bitcast_fusion) | data formatting | bytes 3145728 | tf_op jit(solution)/shard_map/while/body/eval_jaxpr/jit(_where)/select_n | solution.py:78
  189.0 0.0 copy-start.4
  189.0 7.5 %reshape.168 = bf16[3072,256]{1,0:T(8,128)(2,1)S(1)} reshape(bf16[384,8,8,32]{3,2,1,0:T(8,128)(2,1)} %copy.39) | data formatting | bytes 3145728 | tf_op jit(solution)/shard_map/reshape | solution.py:81
  196.5 0.0 copy-done.4
  196.6 2.5 fusion.25
  199.0 40.7 %all_to_all.8 = bf16[384,8,256]{2,1,0:T(8,128)(2,1)S(1)} all-to-all(bf16[384,8,256]{2,1,0:T(8,128)(2,1)S(1)} %fusion.25), channel_id=1, replica_groups=mesh['group'=8,'pos'=4] {'group','pos'}, dimensions={0} | all-to-all | bytes 3145728 | tf_op jit(solution)/shard_map/all_to_all | solution.py:86
  239.7 0.5 bitcast_reduce_fusion
  240.2 0.0 copy-start.6
  240.2 2.0 copy.40
  242.2 0.9 fusion.16
  243.2 0.0 copy-start.8
  243.2 0.1 div.34
  243.4 0.1 rsqrt.25
  243.5 0.0 copy-done.6
  243.5 3.1 %fusion.14 = bf16[3072,256]{1,0:T(8,128)(2,1)S(1)} fusion(f32[32,12,8,256]{3,2,0,1:T(8,128)} %copy.40, f32[256]{0:T(256)S(1)} %copy-done.6, f32[3072]{0:T(1024)S(1)} %rsqrt.25, f32[3072]{0:T(1024)S(1)} %div.34), kind=kLoop, calls=%fused_computation.24 | loop fusion | flops 3145728 | bytes 4744192 | tf_op jit(solution)/shard_map/convert_element_type | solution.py:24
  246.6 0.0 copy-done
  246.6 0.0 copy-done.8
  246.6 6.6 %fusion.10 = bf16[3072,256]{1,0:T(8,128)(2,1)} fusion(f32[3072,256]{1,0:T(8,128)} %bitcast.58, bf16[1024,256]{1,0:T(8,128)(2,1)S(1)} %copy-done, bf16[3072,256]{1,0:T(8,128)(2,1)S(1)} %fusion.14, bf16[256,1024]{1,0:T(8,128)(2,1)S(1)} %copy-done.8), kind=kOutput, calls=%fused_computation.16 | convolution fusion | flops 3229089792 | bytes 7340032 | tf_op jit(solution)/shard_map/dot_general | solution.py:33
  (8 shorter events, 0.1 us)
Async XLA Ops:
  0.0 246.6 %copy-start = (bf16[1024,256]{1,0:T(8,128)(2,1)S(1)}, bf16[1024,256]{1,0:T(8,128)(2,1)}, u32[]{:S(2)}) copy-start(bf16[1024,256]{1,0:T(8,128)(2,1)} %param.19) | copy-start | bytes 1572868
  0.0 10.8 %copy-start.9 = (s32[6]{0:T(128)S(1)}, s32[6]{0:T(128)}, u32[]{:S(2)}) copy-start(s32[6]{0:T(128)} %param.20) | copy-start | bytes 76
  0.0 10.9 %copy-start.7 = (s32[6]{0:T(128)S(1)}, s32[6]{0:T(128)}, u32[]{:S(2)}) copy-start(s32[6]{0:T(128)} %param.21) | copy-start | bytes 76
  3.8 55.4 %all-to-all-start = ((bf16[12,256,256]{2,0,1:T(8,128)(2,1)}), bf16[12,256,256]{2,0,1:T(8,128)(2,1)S(1)}, u32[]{:S(2)}, u32[]{:S(2)}) async-start(bf16[12,256,256]{2,0,1:T(8,128)(2,1)} %copy.33), calls=%async_computation | async-start | bytes 4194304 | tf_op jit(solution)/shard_map/all_to_all | solution.py:47
  61.4 3.1 %copy-start.5 = (f32[256]{0:T(256)S(1)}, f32[256]{0:T(256)}, u32[]{:S(2)}) copy-start(f32[256]{0:T(256)} %param.12) | copy-start | bytes 3076
  64.3 3.3 %copy-start.1 = (bf16[256,256]{1,0:T(8,128)(2,1)S(1)}, bf16[256,256]{1,0:T(8,128)(2,1)}, u32[]{:S(2)}) copy-start(bf16[256,256]{1,0:T(8,128)(2,1)} %param.13) | copy-start | bytes 393220
  69.4 7.9 %copy-start.2 = (bf16[256,256]{1,0:T(8,128)(2,1)S(1)}, bf16[256,256]{1,0:T(8,128)(2,1)}, u32[]{:S(2)}) copy-start(bf16[256,256]{1,0:T(8,128)(2,1)} %param.14) | copy-start | bytes 393220
  78.9 7.9 %copy-start.3 = (bf16[256,256]{1,0:T(8,128)(2,1)S(1)}, bf16[256,256]{1,0:T(8,128)(2,1)}, u32[]{:S(2)}) copy-start(bf16[256,256]{1,0:T(8,128)(2,1)} %param.15) | copy-start | bytes 393220
  189.0 7.6 %copy-start.4 = (bf16[256,256]{1,0:T(8,128)(2,1)S(1)}, bf16[256,256]{1,0:T(8,128)(2,1)}, u32[]{:S(2)}) copy-start(bf16[256,256]{1,0:T(8,128)(2,1)} %param.16) | copy-start | bytes 393220
  240.2 3.3 %copy-start.6 = (f32[256]{0:T(256)S(1)}, f32[256]{0:T(256)}, u32[]{:S(2)}) copy-start(f32[256]{0:T(256)} %param.17) | copy-start | bytes 3076
  243.2 3.4 %copy-start.8 = (bf16[256,1024]{1,0:T(8,128)(2,1)S(1)}, bf16[256,1024]{1,0:T(8,128)(2,1)}, u32[]{:S(2)}) copy-start(bf16[256,1024]{1,0:T(8,128)(2,1)} %param.18) | copy-start | bytes 1572868
where the time goes:
time: 254 us; the launch traced here: 253 us
  other arithmetic  55.9 us (22%)
  matrix products  54.6 us (21%)
  waiting for transfers between devices  48 us (19%)
  local copies, waits for them, and re-layouts  46.7 us (18%)
  blocking collectives  40.7 us (16%)
  starting transfers between devices  7.08 us (3%)
    all_to_all x1, waiting for transfers between devices, local(): lax.all_to_all(features, ('group', 'pos'), split_axis=1, concat_axis=0, t...  48 us
    sub x1, other arithmetic, attend(): exponent = jnp.exp(scores - highest)  42.9 us
    all_to_all x1, blocking collectives, local(): lax.all_to_all(middle, ('group', 'pos'), split_axis=0, concat_axis=1, til...  40.7 us
    reshape x3, local copies, waits for them, and re-layouts, project(): return product.reshape(slots_total, owned, HEADS, head_dim)  23.6 us
    dot_general x1, matrix products, attend(): jnp.einsum('qphe,kphe->phqk', block_query, keys, preferred_element_type=j...  22.9 us
    dot_general x1, matrix products, attend(): jnp.einsum('phqk,kphe->qphe', weights, values, preferred_element_type=jnp...  17.4 us
    select_n x1, local copies, waits for them, and re-layouts, attend(): jnp.where((block_labels >= 0)[:, None, None, None], context, jnp.zeros_li...  9.28 us
    reshape x1, local copies, waits for them, and re-layouts, local(): context = lax.map(attend, starts).reshape(slots_total * owned, width)  7.55 us
  transfers between devices with their start and end apart: 1, of which 1 were waited for; matrix products, arithmetic and copies ran while one was open for 0% of the time, Pallas kernels for 0%

commit v1 on v0

--- a/solution.py
+++ b/solution.py
@@ -44,7 +44,15 @@
     slots_total = local_groups * group_devices * pos_devices
     head_dim = width // HEADS
     scale = 1.0 / math.sqrt(head_dim)
-    gathered = lax.all_to_all(features, ("group", "pos"), split_axis=1, concat_axis=0, tiled=True)
+    gathered = jnp.concatenate(
+        lax.all_to_all(
+            jnp.stack(jnp.split(features, lax.axis_size(("group", "pos")), axis=1)),
+            ("group", "pos"),
+            0,
+            0,
+        ),
+        0,
+    )
     owned = gathered.shape[1]
     labels = segment_ids(counts, offsets, slots_total)
     flat = gathered.reshape(slots_total * owned, width)

time: 254 us -> 288 us (1.13)
  local copies, waits for them, and re-layouts: 46.7 us -> 91.2 us
  waiting for transfers between devices: 48 us -> 37.1 us
  other arithmetic: 55.9 us -> 50.9 us
  matrix products: 54.6 us -> 58 us
    unnamed x21 -> x53, local copies, waits for them, and re-layouts: 3.79 us -> 45.3 us
    all_to_all x1, waiting for transfers between devices: 48 us -> 37.1 us  [local(): lax.all_to_all(jnp.stack(jnp.split(features, lax.axis_size(('group', 'pos...]
where the time goes in v1:
time: 288 us; the launch traced here: 285 us
  local copies, waits for them, and re-layouts  91.2 us (32%)
  matrix products  58 us (20%)
  other arithmetic  50.9 us (18%)
  blocking collectives  40.7 us (14%)
  waiting for transfers between devices  37.1 us (13%)
  starting transfers between devices  7.08 us (2%)
    unnamed x53, local copies, waits for them, and re-layouts  45.3 us
    sub x1, other arithmetic, attend(): exponent = jnp.exp(scores - highest)  42.9 us
    all_to_all x1, blocking collectives, local(): lax.all_to_all(middle, ('group', 'pos'), split_axis=0, concat_axis=1, til...  40.7 us
    all_to_all x1, waiting for transfers between devices, local(): lax.all_to_all(jnp.stack(jnp.split(features, lax.axis_size(('group', 'pos...  37.1 us
    reshape x3, local copies, waits for them, and re-layouts, project(): return product.reshape(slots_total, owned, HEADS, head_dim)  23.6 us
    dot_general x1, matrix products, attend(): jnp.einsum('qphe,kphe->phqk', block_query, keys, preferred_element_type=j...  22.9 us
    dot_general x1, matrix products, attend(): jnp.einsum('phqk,kphe->qphe', weights, values, preferred_element_type=jnp...  18.5 us
    select_n x1, local copies, waits for them, and re-layouts, attend(): jnp.where((block_labels >= 0)[:, None, None, None], context, jnp.zeros_li...  9.94 us
  transfers between devices with their start and end apart: 1, of which 1 were waited for; matrix products, arithmetic and copies ran while one was open for 0% of the time, Pallas kernels for 0%

profile of v1, /device:TPU:1, one launch (start us, length us, event | category | flops | bytes accessed | tf_op | source)
XLA Modules:
  0.0 285.2 jit_solution(11395651524798161817)
XLA Ops:
  0.0 1.5 constant_dynamic-update-slice_fusion.31
  1.5 1.4 constant_dynamic-update-slice_fusion.30
  2.9 1.4 constant_dynamic-update-slice_fusion.29
  4.3 1.4 constant_dynamic-update-slice_fusion.28
  5.7 1.4 constant_dynamic-update-slice_fusion.27
  7.2 1.4 constant_dynamic-update-slice_fusion.26
  8.6 1.4 constant_dynamic-update-slice_fusion.25
  10.0 1.4 constant_dynamic-update-slice_fusion.24
  11.4 1.4 constant_dynamic-update-slice_fusion.23
  12.9 1.4 constant_dynamic-update-slice_fusion.22
  14.3 1.4 constant_dynamic-update-slice_fusion.21
  15.7 1.4 constant_dynamic-update-slice_fusion.20
  17.1 1.4 constant_dynamic-update-slice_fusion.19
  18.5 1.4 constant_dynamic-update-slice_fusion.18
  20.0 1.4 constant_dynamic-update-slice_fusion.17
  21.4 1.4 constant_dynamic-update-slice_fusion.16
  22.8 1.4 constant_dynamic-update-slice_fusion.15
  24.2 1.4 constant_dynamic-update-slice_fusion.14
  25.6 1.4 constant_dynamic-update-slice_fusion.13
  27.1 1.4 constant_dynamic-update-slice_fusion.12
  28.5 1.4 constant_dynamic-update-slice_fusion.11
  29.9 1.4 constant_dynamic-update-slice_fusion.10
  31.3 1.4 constant_dynamic-update-slice_fusion.9
  32.7 1.4 constant_dynamic-update-slice_fusion.8
  34.2 1.4 constant_dynamic-update-slice_fusion.7
  35.6 1.4 constant_dynamic-update-slice_fusion.6
  37.0 1.4 constant_dynamic-update-slice_fusion.5
  38.4 1.4 constant_dynamic-update-slice_fusion.4
  39.9 1.4 constant_dynamic-update-slice_fusion.3
  41.3 1.4 constant_dynamic-update-slice_fusion.2
  42.7 1.4 constant_dynamic-update-slice_fusion.1
  44.1 1.4 constant_dynamic-update-slice_fusion
  45.5 7.1 %all-to-all-start = ((bf16[32,12,8,256]{3,2,1,0:T(8,128)(2,1)}), bf16[32,12,8,256]{3,2,1,0:T(8,128)(2,1)S(1)}, u32[]{:S(2)}, u32[]{:S(2)}) async-start(bf16[32,12,8,256]{3,2,1,0:T(8,128)(2,1)} %constant_dynamic-update-slice_fusion), calls=%async_computation | async-start | bytes 3145728 | tf_op jit(solution)/shard_map/all_to_all | solution.py:48
  52.7 0.1 select_reduce_fusion
  52.8 0.2 compare_and_fusion
  52.9 37.1 %all-to-all-done = bf16[32,12,8,256]{3,2,1,0:T(8,128)(2,1)S(1)} async-done(((bf16[32,12,8,256]{3,2,1,0:T(8,128)(2,1)}), bf16[32,12,8,256]{3,2,1,0:T(8,128)(2,1)S(1)}, u32[]{:S(2)}, u32[]{:S(2)}) %all-to-all-start) | async-done | bytes 1572896 | tf_op jit(solution)/shard_map/all_to_all | solution.py:48
  90.0 0.5 convert_reduce_fusion
  90.5 0.1 div.29
  90.7 0.9 multiply_reduce_fusion
  91.6 0.1 rsqrt.23
  91.8 0.0 copy-start.2
  91.8 1.7 fusion.19
  93.5 0.0 copy-start.1
  93.5 1.1 copy-done.1
  94.6 1.7 convolution_convert_fusion.1
  96.3 7.9 %reshape.160 = bf16[384,8,8,32]{3,2,1,0:T(8,128)(2,1)} reshape(bf16[3072,256]{1,0:T(8,128)(2,1)} %convolution_convert_fusion.1) | data formatting | bytes 3145728 | tf_op jit(solution)/shard_map/reshape | solution.py:63
  104.2 3.1 %convolution_convert_fusion = bf16[3072,256]{1,0:T(8,128)(2,1)} fusion(bf16[3072,256]{1,0:T(8,128)(2,1)} %copy-done.1, bf16[256,256]{1,0:T(8,128)(2,1)S(1)} %copy-done.3), kind=kOutput, calls=%fused_computation.18 | convolution fusion | flops 403439616 | bytes 3276800 | tf_op jit(solution)/shard_map/dot_general | solution.py:62
  107.4 7.9 %reshape.161 = bf16[384,8,8,32]{3,2,1,0:T(8,128)(2,1)} reshape(bf16[3072,256]{1,0:T(8,128)(2,1)} %convolution_convert_fusion) | data formatting | bytes 3145728 | tf_op jit(solution)/shard_map/reshape | solution.py:63
  115.2 3.1 %convolution_convert_fusion.2 = bf16[3072,256]{1,0:T(8,128)(2,1)} fusion(bf16[3072,256]{1,0:T(8,128)(2,1)} %copy-done.1, bf16[256,256]{1,0:T(8,128)(2,1)S(1)} %copy-done.4), kind=kOutput, calls=%fused_computation.20 | convolution fusion | flops 403439616 | bytes 3276800 | tf_op jit(solution)/shard_map/dot_general | solution.py:62
  118.4 7.9 %reshape.159 = bf16[384,8,8,32]{3,2,1,0:T(8,128)(2,1)} reshape(bf16[3072,256]{1,0:T(8,128)(2,1)} %convolution_convert_fusion.2) | data formatting | bytes 3145728 | tf_op jit(solution)/shard_map/reshape | solution.py:63
  126.2 22.9 %fusion.7 = f32[8,8,384,384]{2,3,1,0:T(8,128)} fusion(bf16[384,8,8,32]{3,2,1,0:T(8,128)(2,1)} %reshape.161, bf16[384,8,8,32]{3,2,1,0:T(8,128)(2,1)} %reshape.160), kind=kOutput, calls=%fused_computation.11 | convolution fusion | flops 603979776 | bytes 40894464 | tf_op jit(solution)/shard_map/while/body/eval_jaxpr/qphe,kphe->phqk/dot_general | solution.py:74
  149.2 42.9 %fusion.30 = (f32[8,8,384]{2,1,0:T(8,128)S(1)}, f32[8,8,384,384]{2,3,1,0:T(8,128)}) fusion(f32[8,8,384,384]{2,3,1,0:T(8,128)} %fusion.7, pred[384,384]{0,1:T(8,128)(4,1)S(1)} %compare_and_fusion), kind=kOutput, calls=%fused_computation.85 | output fusion | flops 56623488 | bytes 75743232 | tf_op jit(solution)/shard_map/while/body/eval_jaxpr/sub | solution.py:80
  192.1 18.5 %select_bitcast_fusion = bf16[384,8,8,32]{0,3,2,1:T(8,128)(2,1)} fusion(pred[384]{0:T(512)(128)(4,1)S(1)} %broadcast_compare_fusion, f32[8,8,384,384]{2,3,1,0:T(8,128)} %get-tuple-element.16, f32[8,8,384]{2,1,0:T(8,128)S(1)} %get-tuple-element.15, bf16[384,8,8,32]{3,2,1,0:T(8,128)(2,1)} %reshape.159), kind=kOutput, calls=%fused_computation.36 | convolution fusion | flops 624427008 | bytes 40993152 | tf_op jit(solution)/shard_map/while/body/eval_jaxpr/phqk,kphe->qphe/dot_general | solution.py:83
  210.6 9.9 %copy.27 = bf16[384,8,8,32]{3,2,1,0:T(8,128)(2,1)} copy(bf16[384,8,8,32]{0,3,2,1:T(8,128)(2,1)} %select_bitcast_fusion) | data formatting | bytes 3145728 | tf_op jit(solution)/shard_map/while/body/eval_jaxpr/jit(_where)/select_n | solution.py:86
  220.6 8.4 %reshape.162 = bf16[3072,256]{1,0:T(8,128)(2,1)} reshape(bf16[384,8,8,32]{3,2,1,0:T(8,128)(2,1)} %copy.27) | data formatting | bytes 3145728 | tf_op jit(solution)/shard_map/reshape | solution.py:89
  229.0 2.0 fusion.23
  231.0 40.7 %all_to_all.14 = bf16[384,8,256]{2,1,0:T(8,128)(2,1)S(1)} all-to-all(bf16[384,8,256]{2,1,0:T(8,128)(2,1)S(1)} %fusion.23), channel_id=1, replica_groups=mesh['group'=8,'pos'=4] {'group','pos'}, dimensions={0} | all-to-all | bytes 3145728 | tf_op jit(solution)/shard_map/all_to_all | solution.py:94
  271.7 0.5 bitcast_reduce_fusion
  272.2 2.0 copy.28
  274.2 0.9 fusion.16
  275.1 0.1 div.34
  275.3 0.1 rsqrt.25
  275.4 3.1 %fusion.14 = bf16[3072,256]{1,0:T(8,128)(2,1)S(1)} fusion(f32[32,12,8,256]{3,2,0,1:T(8,128)} %copy.28, f32[256]{0:T(256)S(1)} %copy-done.7, f32[3072]{0:T(1024)S(1)} %rsqrt.25, f32[3072]{0:T(1024)S(1)} %div.34), kind=kLoop, calls=%fused_computation.24 | loop fusion | flops 3145728 | bytes 4744192 | tf_op jit(solution)/shard_map/convert_element_type | solution.py:24
  278.6 6.6 %fusion.10 = bf16[3072,256]{1,0:T(8,128)(2,1)} fusion(f32[3072,256]{1,0:T(8,128)} %bitcast.113, bf16[1024,256]{1,0:T(8,128)(2,1)S(1)} %copy-done, bf16[3072,256]{1,0:T(8,128)(2,1)S(1)} %fusion.14, bf16[256,1024]{1,0:T(8,128)(2,1)S(1)} %copy-done.9), kind=kOutput, calls=%fused_computation.16 | convolution fusion | flops 3229089792 | bytes 7340032 | tf_op jit(solution)/shard_map/dot_general | solution.py:33
  (27 shorter events, 0.2 us)
Async XLA Ops:
  0.0 278.6 %copy-start = (bf16[1024,256]{1,0:T(8,128)(2,1)S(1)}, bf16[1024,256]{1,0:T(8,128)(2,1)}, u32[]{:S(2)}) copy-start(bf16[1024,256]{1,0:T(8,128)(2,1)} %param.19) | copy-start | bytes 1572868
  45.5 7.1 %copy-start.8 = (s32[6]{0:T(128)S(1)}, s32[6]{0:T(128)}, u32[]{:S(2)}) copy-start(s32[6]{0:T(128)} %param.21) | copy-start | bytes 76
  45.5 7.1 %copy-start.10 = (s32[6]{0:T(128)S(1)}, s32[6]{0:T(128)}, u32[]{:S(2)}) copy-start(s32[6]{0:T(128)} %param.20) | copy-start | bytes 76
  45.5 44.5 %all-to-all-start = ((bf16[32,12,8,256]{3,2,1,0:T(8,128)(2,1)}), bf16[32,12,8,256]{3,2,1,0:T(8,128)(2,1)S(1)}, u32[]{:S(2)}, u32[]{:S(2)}) async-start(bf16[32,12,8,256]{3,2,1,0:T(8,128)(2,1)} %constant_dynamic-update-slice_fusion), calls=%async_computation | async-start | bytes 3145728 | tf_op jit(solution)/shard_map/all_to_all | solution.py:48
  90.5 1.2 copy-start.6
  91.8 2.8 copy-start.2
  93.5 1.1 copy-start.1
  96.3 7.9 %copy-start.3 = (bf16[256,256]{1,0:T(8,128)(2,1)S(1)}, bf16[256,256]{1,0:T(8,128)(2,1)}, u32[]{:S(2)}) copy-start(bf16[256,256]{1,0:T(8,128)(2,1)} %param.14) | copy-start | bytes 393220
  107.4 7.9 %copy-start.4 = (bf16[256,256]{1,0:T(8,128)(2,1)S(1)}, bf16[256,256]{1,0:T(8,128)(2,1)}, u32[]{:S(2)}) copy-start(bf16[256,256]{1,0:T(8,128)(2,1)} %param.15) | copy-start | bytes 393220
  220.6 8.4 %copy-start.5 = (bf16[256,256]{1,0:T(8,128)(2,1)S(1)}, bf16[256,256]{1,0:T(8,128)(2,1)}, u32[]{:S(2)}) copy-start(bf16[256,256]{1,0:T(8,128)(2,1)} %param.16) | copy-start | bytes 393220
  274.1 1.3 copy-start.7
  275.4 3.2 %copy-start.9 = (bf16[256,1024]{1,0:T(8,128)(2,1)S(1)}, bf16[256,1024]{1,0:T(8,128)(2,1)}, u32[]{:S(2)}) copy-start(bf16[256,1024]{1,0:T(8,128)(2,1)} %param.18) | copy-start | bytes 1572868
